TPU v7x, 32 devices: a whole 2x2x4 slice. The times are simulated.
32 devices in a mesh: group: 2 (over x), dp: 4 (over y, core), tensor: 4 (over z).
Axes of the slice: x: 2, y: 2, z: 4, core: 2. Of those that a mesh axis runs over, the one named last changes fastest.
Arguments:
- tokens: bfloat16 [1024, 5120], P(('group', 'dp'), 'tensor'), parts along dimension 0, may hold values from -6 to 6
- router: bfloat16 [5120, 2], replicated, may hold values from -0.078125 to 0.078125
- expert_gate: bfloat16 [5120, 8192], P(None, ('dp', 'tensor')), may hold values from -0.078125 to 0.078125
- expert_up: bfloat16 [5120, 8192], P(None, ('dp', 'tensor')), may hold values from -0.078125 to 0.078125
- expert_down: bfloat16 [8192, 5120], P(('dp', 'tensor')), may hold values from -0.09375 to 0.09375
- shared_gate: bfloat16 [5120, 4096], P('dp', 'tensor'), may hold values from -0.078125 to 0.078125
- shared_up: bfloat16 [5120, 4096], P('dp', 'tensor'), may hold values from -0.078125 to 0.078125
- shared_down: bfloat16 [4096, 5120], P('tensor', 'dp'), may hold values from -0.09375 to 0.09375
- expert_ids: int32 [1024], P(('group', 'dp')), parts along dimension 0, may hold values from 0 to 1, as said below
- expert_slots: int32 [1024], P(('group', 'dp')), parts along dimension 0, may hold values from 0 to 63, as said below
Outputs:
- mixed: bfloat16 [1024, 5120], P(('group', 'dp'), 'tensor'), parts along dimension 0
There are 2 independent parts, one for each index of `group`. A program takes and returns all parts, laid end to end along the dimension named above; an argument that names none is the same for every part. Nothing has to cross between parts.
Inputs may be any that keep to these rules, and one draw needn't show every extreme that they name: `expert_ids`: among the tokens of one index of dp no expert has more than 64; in every draw one expert has exactly 64 tokens from every index of dp. `expert_slots`: tokens of one index of dp with the same expert have distinct slots.
All inputs are finite; a program needn't handle non-finite values.
Results may differ from a plain program's by a relative error of at most 0.015.
Values may be sent and summed in bfloat16 or wider, within the bound.
A program may use at most 128 MiB of HBM per device.

v0:
```python
import jax
import jax.numpy as jnp
from jax import lax
from jax.sharding import PartitionSpec as P


def on_device(
    tokens,
    router,
    expert_gate,
    expert_up,
    expert_down,
    shared_gate,
    shared_up,
    shared_down,
    expert_ids,
    expert_slots,
):
    tok_rows, part_width = tokens.shape
    dp_count = lax.axis_size("dp")
    experts = dp_count // 2
    capacity = min(2 * tok_rows // experts, tok_rows // 2)
    gathered = lax.all_gather(tokens, "tensor", axis=1, tiled=True)
    logits = jnp.dot(gathered, router, preferred_element_type=jnp.float32)
    one_hot = (expert_ids[:, None] == jnp.arange(experts, dtype=jnp.int32)[None, :]).astype(
        jnp.float32
    )
    gating = jax.nn.sigmoid(jnp.sum(logits * one_hot, axis=1))
    routed = (tokens.astype(jnp.float32) * gating[:, None]).astype(jnp.bfloat16)
    outgoing = (
        jnp.zeros((experts, capacity, part_width), jnp.bfloat16)
        .at[expert_ids, expert_slots]
        .set(routed)
    )
    gate_sum = jnp.dot(
        gathered,
        lax.all_gather(shared_gate, "dp", axis=0, tiled=True),
        preferred_element_type=jnp.float32,
    )
    up_sum = jnp.dot(
        gathered,
        lax.all_gather(shared_up, "dp", axis=0, tiled=True),
        preferred_element_type=jnp.float32,
    )
    shared_hidden = (jax.nn.silu(gate_sum) * up_sum).astype(jnp.bfloat16)
    shared_terms = jnp.dot(
        shared_hidden,
        lax.all_gather(shared_down, "dp", axis=1, tiled=True),
        preferred_element_type=jnp.float32,
    )
    shared_out = lax.psum_scatter(
        shared_terms.astype(jnp.bfloat16), "tensor", scatter_dimension=1, tiled=True
    ).astype(jnp.float32)
    to_send = jnp.repeat(outgoing, 2, axis=0)
    received = lax.all_to_all(to_send, "dp", split_axis=0, concat_axis=0, tiled=True)
    source_count = received.shape[0]
    slot_count = received.shape[1]
    slot_total = source_count * slot_count
    portion = lax.all_gather(received, "tensor", axis=2, tiled=True)
    flattened = portion.reshape(slot_total, portion.shape[2])
    gate_e = jnp.dot(flattened, expert_gate, preferred_element_type=jnp.float32)
    up_e = jnp.dot(flattened, expert_up, preferred_element_type=jnp.float32)
    hidden_e = (jax.nn.silu(gate_e) * up_e).astype(jnp.bfloat16)
    expert_terms = jnp.dot(hidden_e, expert_down, preferred_element_type=jnp.float32)
    expert_terms = expert_terms.reshape(source_count, slot_count, expert_terms.shape[1])
    returned_raw = lax.all_to_all(
        lax.psum_scatter(
            expert_terms.astype(jnp.bfloat16), "tensor", scatter_dimension=2, tiled=True
        ),
        "dp",
        split_axis=0,
        concat_axis=0,
        tiled=True,
    ).astype(jnp.float32)
    returned = (
        returned_raw.reshape(experts, 2, capacity, part_width).sum(axis=1).astype(jnp.bfloat16)
    )
    expert_out = returned[expert_ids, expert_slots]
    return (shared_out + expert_out.astype(jnp.float32)).astype(jnp.bfloat16)


def solution(mesh):
    in_specs = (
        P(("group", "dp"), "tensor"),
        P(),
        P(None, ("dp", "tensor")),
        P(None, ("dp", "tensor")),
        P(("dp", "tensor"), None),
        P("dp", "tensor"),
        P("dp", "tensor"),
        P("tensor", "dp"),
        P(("group", "dp")),
        P(("group", "dp")),
    )
    out_specs = P(("group", "dp"), "tensor")
    return jax.shard_map(
        on_device, mesh=mesh, in_specs=in_specs, out_specs=out_specs, check_vma=False
    )
```

profile of v0, /device:TPU:1, one launch (start us, length us, event | category | flops | bytes accessed | tf_op | source)
XLA Modules:
  0.0 432.5 jit_solution(5085881878389791169)
XLA Ops:
  6.5 0.7 all-gather.6.cloned.1.call-update
  7.3 0.7 fusion.19
  8.0 34.8 %all-gather.6.cloned.1.call-done = bf16[128,5120]{1,0:T(8,128)(2,1)} async-done(((bf16[128,1280]{1,0:T(8,128)(2,1)}), bf16[128,5120]{1,0:T(8,128)(2,1)}) %all-gather.6.cloned.1.call-update) | async-done | bytes 1310736 | tf_op jit(solution)/shard_map/all_gather | solution.py:23
  42.8 1.8 fusion.2
  44.6 1.1 multiply_convert_fusion
  45.8 9.8 %scatter_fusion = bf16[2,64,1280]{2,1,0:T(8,128)(2,1)S(1)} fusion(bf16[2,64,1280]{2,1,0:T(8,128)(2,1)S(1)} %broadcast_in_dim.8, s32[128]{0:T(128)S(1)} %get-tuple-element.6, bf16[128,1280]{1,0:T(8,128)(2,1)S(1)} %multiply_convert_fusion), kind=kCustom, calls=%fused_computation.1 | custom fusion | bytes 984064 | tf_op jit(solution)/shard_map/scatter | solution.py:33
  55.6 13.7 %all_to_all.10 = bf16[4,64,1280]{2,1,0:T(8,128)(2,1)} all-to-all(bf16[4,64,1280]{2,1,0:T(8,128)(2,1)S(1)} %bitcast.42), channel_id=1, replica_groups=mesh['group'=2,'dp'=4,'tensor'=4] {'dp'}, dimensions={0} | all-to-all | bytes 1310720 | tf_op jit(solution)/shard_map/all_to_all | solution.py:55
  69.4 0.7 all-gather.8.cloned.1.call-update
  70.1 0.5 all-gather.10.cloned.1.call-update
  70.7 0.5 all-gather.12.cloned.1.call-update
  71.3 51.3 %all-gather.14.cloned.1.call-done = bf16[4,64,5120]{2,1,0:T(8,128)(2,1)} async-done(((bf16[4,64,1280]{2,1,0:T(8,128)(2,1)}), bf16[4,64,5120]{2,1,0:T(8,128)(2,1)}) %all-gather.14.cloned.1.call-update) | async-done | bytes 2621456 | tf_op jit(solution)/shard_map/all_gather | solution.py:59
  122.6 4.8 %fusion.23 = f32[256,512]{1,0:T(8,128)S(1)} fusion(bf16[256,5120]{1,0:T(8,128)(2,1)} %bitcast.43, bf16[5120,512]{1,0:T(8,128)(2,1)} %param.12), kind=kOutput, calls=%fused_computation.39 | convolution fusion | flops 1342177280 | bytes 8388608 | tf_op jit(solution)/shard_map/dot_general | solution.py:61
  127.4 10.8 %convolution_convert_fusion = bf16[256,5120]{1,0:T(8,128)(2,1)} fusion(bf16[512,5120]{1,0:T(8,128)(2,1)} %param.14, bf16[256,5120]{1,0:T(8,128)(2,1)} %bitcast.44, bf16[5120,512]{1,0:T(8,128)(2,1)} %param.13, f32[256,512]{1,0:T(8,128)S(1)} %fusion.23), kind=kOutput, calls=%fused_computation.2 | convolution fusion | flops 2686451712 | bytes 16252928 | tf_op jit(solution)/shard_map/dot_general | solution.py:64
  138.3 55.4 %all-gather.8.cloned.1.call-done = bf16[5120,1024]{1,0:T(8,128)(2,1)} async-done(((bf16[1280,1024]{1,0:T(8,128)(2,1)}), bf16[5120,1024]{1,0:T(8,128)(2,1)}) %all-gather.8.cloned.1.call-update) | async-done | bytes 10485776 | tf_op jit(solution)/shard_map/all_gather | solution.py:37
  193.8 5.6 %fusion.22 = f32[128,1024]{1,0:T(8,128)S(1)} fusion(bf16[128,5120]{1,0:T(8,128)(2,1)S(1)} %copy-done.2, bf16[5120,1024]{1,0:T(8,128)(2,1)} %all-gather.8.cloned.1.call-done), kind=kOutput, calls=%fused_computation.38 | convolution fusion | flops 1342177280 | bytes 12320768 | tf_op jit(solution)/shard_map/dot_general | solution.py:35
  199.4 66.0 %all-gather.10.cloned.1.call-done = bf16[5120,1024]{1,0:T(8,128)(2,1)} async-done(((bf16[1280,1024]{1,0:T(8,128)(2,1)}), bf16[5120,1024]{1,0:T(8,128)(2,1)}) %all-gather.10.cloned.1.call-update) | async-done | bytes 10485776 | tf_op jit(solution)/shard_map/all_gather | solution.py:42
  265.4 71.6 %all-gather.12.cloned.1.call-done = bf16[1024,5120]{1,0:T(8,128)(2,1)} async-done(((bf16[1024,1280]{1,0:T(8,128)(2,1)}), bf16[1024,5120]{1,0:T(8,128)(2,1)}) %all-gather.12.cloned.1.call-update) | async-done | bytes 10485776 | tf_op jit(solution)/shard_map/all_gather | solution.py:48
  337.0 11.2 %convolution_convert_fusion.1 = bf16[128,5120]{1,0:T(8,128)(2,1)} fusion(bf16[1024,5120]{1,0:T(8,128)(2,1)} %all-gather.12.cloned.1.call-done, bf16[128,5120]{1,0:T(8,128)(2,1)S(1)} %copy-done.2, bf16[5120,1024]{1,0:T(8,128)(2,1)} %all-gather.10.cloned.1.call-done, f32[128,1024]{1,0:T(8,128)S(1)} %fusion.22), kind=kOutput, calls=%fused_computation.3 | convolution fusion | flops 2685796352 | bytes 24117248 | tf_op jit(solution)/shard_map/dot_general | solution.py:46
  348.2 42.4 %reduce-scatter.5.cloned.1.call-done = bf16[4,64,1280]{2,1,0:T(8,128)(2,1)} async-done(((bf16[4,64,5120]{2,1,0:T(8,128)(2,1)}), bf16[4,64,1280]{2,1,0:T(8,128)(2,1)}) %reduce-scatter.5.cloned.1.call-update) | async-done | bytes 655376 | tf_op jit(solution)/shard_map/reduce_scatter | solution.py:67
  390.6 14.1 %all_to_all.11 = bf16[4,64,1280]{2,1,0:T(8,128)(2,1)S(1)} all-to-all(bf16[4,64,1280]{2,1,0:T(8,128)(2,1)} %reduce-scatter.5.cloned.1.call-done), channel_id=1, replica_groups=mesh['group'=2,'dp'=4,'tensor'=4] {'dp'}, dimensions={0} | all-to-all | bytes 1310720 | tf_op jit(solution)/shard_map/all_to_all | solution.py:66
  404.7 0.1 bitcast_reduce_fusion
  404.8 1.9 gather_fusion
  406.7 17.2 %reduce-scatter.3.cloned.1.call-done = bf16[128,1280]{1,0:T(8,128)(2,1)} async-done(((bf16[128,5120]{1,0:T(8,128)(2,1)}), bf16[128,1280]{1,0:T(8,128)(2,1)}) %reduce-scatter.3.cloned.1.call-update) | async-done | bytes 327696 | tf_op jit(solution)/shard_map/reduce_scatter | solution.py:51
  423.9 1.8 add_convert_fusion
  (19 shorter events, 0.4 us)
Async XLA Ops:
  6.5 36.3 %copy-start = (bf16[5120,2]{0,1:T(2,128)(2,1)S(1)}, bf16[5120,2]{0,1:T(2,128)(2,1)}, u32[]{:S(2)}) copy-start(bf16[5120,2]{0,1:T(2,128)(2,1)} %param.11) | copy-start | bytes 61444
  6.5 36.3 %all-gather.6.cloned.1.call-start = ((), (), s32[]{:S(2)}) async-start(), calls=%async_computation.4 | async-start | bytes 1638400 | tf_op jit(solution)/shard_map/all_gather | solution.py:23
  7.3 115.4 %all-gather.14.cloned.1.call-start = ((), (), s32[]{:S(2)}) async-start(), calls=%async_computation.9 | async-start | bytes 3276800 | tf_op jit(solution)/shard_map/all_gather | solution.py:59
  69.3 124.4 %all-gather.8.cloned.1.call-start = ((), (), s32[]{:S(2)}) async-start(), calls=%async_computation.5 | async-start | bytes 13107200 | tf_op jit(solution)/shard_map/all_gather | solution.py:37
  70.1 195.3 %all-gather.10.cloned.1.call-start = ((), (), s32[]{:S(2)}) async-start(), calls=%async_computation.6 | async-start | bytes 13107200 | tf_op jit(solution)/shard_map/all_gather | solution.py:42
  70.7 266.3 %all-gather.12.cloned.1.call-start = ((), (), s32[]{:S(2)}) async-start(), calls=%async_computation.7 | async-start | bytes 13107200 | tf_op jit(solution)/shard_map/all_gather | solution.py:48
  71.2 319.4 %reduce-scatter.5.cloned.1.call-start = ((), (), s32[]{:S(2)}) async-start(), calls=%async_computation.10 | async-start | bytes 3276800 | tf_op jit(solution)/shard_map/reduce_scatter | solution.py:67
  127.4 66.3 %copy-start.2 = (bf16[128,5120]{1,0:T(8,128)(2,1)S(1)}, bf16[128,5120]{1,0:T(8,128)(2,1)}, u32[]{:S(2)}) copy-start(bf16[128,5120]{1,0:T(8,128)(2,1)} %all-gather.6.cloned.1.call-done) | copy-start | bytes 3932164
  138.3 285.6 %reduce-scatter.3.cloned.1.call-start = ((), (), s32[]{:S(2)}) async-start(), calls=%async_computation.8 | async-start | bytes 1638400 | tf_op jit(solution)/shard_map/reduce_scatter | solution.py:51
  337.0 88.7 %copy-start.1 = (bf16[5120,2]{0,1:T(2,128)(2,1)S(1)}, bf16[5120,2]{0,1:T(2,128)(2,1)}, u32[]{:S(2)}) copy-start(bf16[5120,2]{0,1:T(2,128)(2,1)} %param.11) | copy-start | bytes 61444
Sparse Core Ops, SparseCore 0:
  8.9 33.8 all-gather.5
  69.5 53.1 all-gather.13
  124.2 69.5 all-gather.7
  195.2 70.1 all-gather.9
  266.8 70.1 all-gather.11
  339.1 51.4 reduce-scatter.4
  392.9 30.9 reduce-scatter.2
where the time goes:
time: 434 us; the launch traced here: 433 us
  waiting for transfers between devices  341 us (79%)
  matrix products  34.2 us (8%)
  blocking collectives  27.8 us (6%)
  between operations  13.6 us (3%)
  local copies, waits for them, and re-layouts  11.8 us (3%)
    all_gather x1, waiting for transfers between devices, on_device(): lax.all_gather(shared_down, 'dp', axis=1, tiled=True)  71.6 us
    all_gather x1, waiting for transfers between devices, on_device(): lax.all_gather(shared_up, 'dp', axis=0, tiled=True)  66 us
    all_gather x1, waiting for transfers between devices, on_device(): lax.all_gather(shared_gate, 'dp', axis=0, tiled=True)  55.4 us
    all_gather x1, waiting for transfers between devices, on_device(): portion = lax.all_gather(received, 'tensor', axis=2, tiled=True)  51.3 us
    reduce_scatter x1, waiting for transfers between devices, on_device(): lax.psum_scatter(expert_terms.astype(jnp.bfloat16), 'tensor', scatter_dim...  42.4 us
    all_gather x1, waiting for transfers between devices, on_device(): gathered = lax.all_gather(tokens, 'tensor', axis=1, tiled=True)  34.8 us
    reduce_scatter x1, waiting for transfers between devices, on_device(): lax.psum_scatter(shared_terms.astype(jnp.bfloat16), 'tensor', scatter_dim...  17.2 us
    all_to_all x1, blocking collectives, on_device(): lax.all_to_all(lax.psum_scatter(expert_terms.astype(jnp.bfloat16), 'tenso...  14.1 us
  transfers between devices with their start and end apart: 7, of which 7 were waited for; matrix products, arithmetic and copies ran while one was open for 8% of the time, Pallas kernels for 0%

commit v1 on v0

--- a/solution.py
+++ b/solution.py
@@ -1,6 +1,10 @@
+import functools
+
 import jax
 import jax.numpy as jnp
 from jax import lax
+from jax.experimental import pallas as pl
+from jax.experimental.pallas import tpu as pltpu
 from jax.sharding import PartitionSpec as P
 
 
@@ -79,6 +83,395 @@
     return (shared_out + expert_out.astype(jnp.float32)).astype(jnp.bfloat16)
 
 
+VMEM_BYTES = 64 * 1024 * 1024 - 65536
+
+
+def tile_of(width):
+    return next(t for t in (256, 128, width) if width % t == 0)
+
+
+def layer_kernel(
+    shape,
+    tok, pick, unpick, router,
+    eg_hbm, eu_hbm, ed_hbm, sg_hbm, su_hbm, sd_hbm,
+    out,
+    eg, eu, ed, sg, su, sd,
+    own, table, rest, logit, acc_g, acc_u, hid_e, part_e, core_e, row_e, pair_e,
+    part_s, got_s, hid_s, down_s, gotd_s, left, right, passed,
+    wsem, send_y, recv_y, send_q, recv_q, send_ql, send_qr, send_l, send_r, recv_z, send_c, recv_c,
+    send_pc, recv_pc, send_py, recv_py, send_gs, recv_gs, send_h, recv_h, send_d, recv_d,
+    send_tr, send_tl, recv_tl, recv_tr,
+):
+    ndp, nt, cap, width = shape
+    group, dp, z = (lax.axis_index(n) for n in ("group", "dp", "tensor"))
+    y, c = lax.div(dp, 2), lax.rem(dp, 2)
+    mate, across = 2 * y + 1 - c, 2 * (1 - y) + c
+    others = [lax.rem(dp + i, ndp) for i in range(1, ndp)]
+    rows = ndp * cap
+    sending = []
+
+    def copy(src, dst, ss, rs, dev_dp, dev_z):
+        return pltpu.make_async_remote_copy(
+            src_ref=src, dst_ref=dst, send_sem=ss, recv_sem=rs,
+            device_id=(group, dev_dp, dev_z), device_id_type=pl.DeviceIdType.MESH,
+        )
+
+    def send(cond, make):
+        if cond is None:
+            make().start()
+        else:
+            pl.when(cond)(lambda: make().start())
+        sending.append((cond, make))
+
+    weights = [
+        pltpu.make_async_copy(a, b, wsem.at[i])
+        for i, (a, b) in enumerate(
+            ((sg_hbm, sg), (su_hbm, su), (eg_hbm, eg), (eu_hbm, eu), (ed_hbm, ed), (sd_hbm, sd))
+        )
+    ]
+    for w in weights:
+        w.start()
+
+    barrier = pltpu.get_barrier_semaphore()
+    for o in others:
+        pl.semaphore_signal(barrier, 1, device_id=(group, o, z), device_id_type=pl.DeviceIdType.MESH)
+
+    @pl.when(z > 0)
+    def _():
+        pl.semaphore_signal(barrier, 1, device_id=(group, dp, z - 1), device_id_type=pl.DeviceIdType.MESH)
+
+    @pl.when(z < nt - 1)
+    def _():
+        pl.semaphore_signal(barrier, 1, device_id=(group, dp, z + 1), device_id_type=pl.DeviceIdType.MESH)
+
+    tw = tile_of(width)
+
+    @pl.loop(0, width // tw)
+    def _(i):
+        cols = pl.ds(pl.multiple_of(i * tw, tw), tw)
+        picked = jnp.dot(pick[...], tok[:, cols], preferred_element_type=jnp.float32)
+        own[:, :, cols] = picked.astype(jnp.bfloat16).reshape(2, cap, tw)
+
+    table[z, dp] = own[y]
+
+    @pl.when(dp == z)
+    def _():
+        rest[dp] = own[1 - y]
+
+    at_end = (z == 0) | (z == nt - 1)
+
+    @pl.when(at_end)
+    def _():
+        pl.semaphore_wait(barrier, ndp)
+
+    @pl.when(jnp.logical_not(at_end))
+    def _():
+        pl.semaphore_wait(barrier, ndp + 1)
+
+    send(None, lambda: copy(own.at[1 - y], table.at[z, dp], send_y, recv_y, across, z))
+    home_row = lax.div(z, 2)
+    send(dp != z, lambda: copy(own.at[1 - home_row], rest.at[dp], send_q, recv_q.at[dp], z, z))
+
+    def spread(zs, j, toward_left, toward_right):
+        block = table.at[zs, 2 * j + c]
+        send(toward_right, lambda: copy(block, block, send_r.at[zs, j], recv_z.at[zs, j], dp, z + 1))
+        send(toward_left, lambda: copy(block, block, send_l.at[zs, j], recv_z.at[zs, j], dp, z - 1))
+
+    def to_mate(cond, zs, j):
+        block = table.at[zs, 2 * j + c]
+        send(cond, lambda: copy(block, block, send_c.at[zs, j], recv_c.at[zs, j], mate, z))
+
+    spread(z, y, z > 0, z < nt - 1)
+    to_mate(None, z, y)
+    copy(own.at[0], table.at[z, across], send_y, recv_y, across, z).wait_recv()
+    spread(z, 1 - y, z > 0, z < nt - 1)
+    to_mate(None, z, 1 - y)
+
+    def relay_rest(distance):
+        for s in range(ndp):
+            for at, go_left, go_right in (
+                ((z == dp, z > 0, z < nt - 1),)
+                if distance == 0
+                else (
+                    (z == dp + distance, None, z < nt - 1),
+                    (z == dp - distance, z > 0, None),
+                )
+            ):
+                waits = at & (dp != s) if distance == 0 else at
+
+                @pl.when(waits)
+                def _():
+                    copy(rest.at[s], rest.at[s], send_q, recv_q.at[s], dp, z).wait_recv()
+
+                if go_left is not None:
+                    send(at & go_left, lambda s=s: copy(
+                        rest.at[s], rest.at[s], send_ql.at[s], recv_q.at[s], dp, z - 1))
+                if go_right is not None:
+                    send(at & go_right, lambda s=s: copy(
+                        rest.at[s], rest.at[s], send_qr.at[s], recv_q.at[s], dp, z + 1))
+
+    te = tile_of(acc_g.shape[1])
+
+    logit[...] = jnp.zeros_like(logit)
+    acc_g[...] = jnp.zeros_like(acc_g)
+    acc_u[...] = jnp.zeros_like(acc_u)
+
+    def expert_chunk(zs):
+        for j in range(2):
+            block = table.at[zs, 2 * j + 1 - c]
+            copy(block, block, send_c.at[zs, j], recv_c.at[zs, j], mate, z).wait_recv()
+        depth = pl.ds(pl.multiple_of(zs * width, width), width)
+        x = table.at[zs]
+        logit[...] += jnp.dot(
+            x[...].reshape(rows, width), router[depth, :], preferred_element_type=jnp.float32
+        )
+
+        @pl.loop(0, acc_g.shape[1] // te)
+        def _(i):
+            cols = pl.ds(pl.multiple_of(i * te, te), te)
+            xs = x[...].reshape(rows, width)
+            acc_g[:, cols] += jnp.dot(xs, eg[depth, cols], preferred_element_type=jnp.float32)
+            acc_u[:, cols] += jnp.dot(xs, eu[depth, cols], preferred_element_type=jnp.float32)
+
+    relay_rest(0)
+    for distance in range(1, nt):
+        for zs, inside, far in (
+            (z - distance, z >= distance, "right"),
+            (z + distance, z + distance < nt, "left"),
+        ):
+            for jr in range(2):
+                j = y if jr == 0 else 1 - y
+
+                @pl.when(inside)
+                def _():
+                    block = table.at[zs, 2 * j + c]
+                    copy(block, block, send_r.at[zs, j], recv_z.at[zs, j], dp, z).wait_recv()
+
+                block = lambda zs=zs, j=j: table.at[zs, 2 * j + c]
+                if far == "right":
+                    send(inside & (z < nt - 1), lambda zs=zs, j=j, block=block: copy(
+                        block(), block(), send_r.at[zs, j], recv_z.at[zs, j], dp, z + 1))
+                else:
+                    send(inside & (z > 0), lambda zs=zs, j=j, block=block: copy(
+                        block(), block(), send_l.at[zs, j], recv_z.at[zs, j], dp, z - 1))
+                send(inside, lambda zs=zs, j=j, block=block: copy(
+                    block(), block(), send_c.at[zs, j], recv_c.at[zs, j], mate, z))
+        relay_rest(distance)
+        if distance == 1:
+            for w in weights[:4]:
+                w.wait()
+            expert_chunk(z)
+        else:
+            for zs, inside in ((z - distance + 1, z >= distance - 1), (z + distance - 1, z + distance - 1 < nt)):
+                pl.when(inside)(functools.partial(expert_chunk, zs))
+    last = nt - 1
+    for zs, inside in ((z - last, z >= last), (z + last, z + last < nt)):
+        pl.when(inside)(functools.partial(expert_chunk, zs))
+
+    hs = sg.shape[1]
+    ts = tile_of(hs)
+
+    @pl.loop(0, hs // ts)
+    def _(i):
+        cols = pl.ds(pl.multiple_of(i * ts, ts), ts)
+        for w, k in ((sg, 0), (su, 1)):
+            for src, e in ((table.at[dp], y), (rest, 1 - y)):
+                part = jnp.dot(
+                    src[...].reshape(rows, width), w[:, cols], preferred_element_type=jnp.float32
+                )
+                part_s[:, k, e, :, cols] = part.astype(jnp.bfloat16).reshape(ndp, cap, ts)
+
+    for i, o in enumerate(others):
+        send(None, lambda i=i, o=o: copy(
+            part_s.at[o], got_s.at[i], send_gs.at[i], recv_gs.at[i], o, z))
+
+    lanes = lax.broadcasted_iota(jnp.int32, logit.shape, 1)
+    gating = jax.nn.sigmoid(jnp.sum(jnp.where(lanes == y, logit[...], 0.0), axis=1, keepdims=True))
+    hid_e[...] = (jax.nn.silu(acc_g[...] * gating) * (acc_u[...] * gating)).astype(jnp.bfloat16)
+    weights[4].wait()
+    per = width // tw
+
+    @pl.loop(0, nt * per)
+    def _(i):
+        t, n = lax.div(i, per), lax.rem(i, per)
+        part = jnp.dot(
+            hid_e[...], ed[:, pl.ds(pl.multiple_of(i * tw, tw), tw)],
+            preferred_element_type=jnp.float32,
+        )
+        part_e[:, t, :, pl.ds(pl.multiple_of(n * tw, tw), tw)] = part.astype(
+            jnp.bfloat16
+        ).reshape(ndp, cap, tw)
+
+    for j in range(2):
+        send(None, lambda j=j: copy(
+            part_e.at[2 * j + 1 - c], core_e.at[j], send_pc.at[j], recv_pc.at[j], mate, z))
+
+    for i in range(ndp - 1):
+        copy(part_s.at[0], got_s.at[i], send_gs.at[i], recv_gs.at[i], dp, z).wait_recv()
+
+    @pl.loop(0, hs // ts)
+    def _(i):
+        cols = pl.ds(pl.multiple_of(i * ts, ts), ts)
+        total = part_s[dp, :, :, :, cols].astype(jnp.float32)
+        for k in range(ndp - 1):
+            total = total + got_s[k, :, :, :, cols].astype(jnp.float32)
+        hid_s[dp, :, cols] = (jax.nn.silu(total[0]) * total[1]).astype(jnp.bfloat16).reshape(
+            2 * cap, ts
+        )
+
+    for i, o in enumerate(others):
+        send(None, lambda i=i, o=o: copy(
+            hid_s.at[dp], hid_s.at[dp], send_h.at[i], recv_h.at[dp], o, z))
+
+    for j in range(2):
+        copy(part_e.at[0], core_e.at[j], send_pc.at[j], recv_pc.at[j], dp, z).wait_recv()
+
+    @pl.loop(0, nt)
+    def _(t):
+        both = part_e[across, t].astype(jnp.float32) + core_e[1 - y, t].astype(jnp.float32)
+        pair_e[t] = both.astype(jnp.bfloat16)
+
+    send(None, lambda: copy(pair_e, row_e, send_py, recv_py, across, z))
+
+    for o in others:
+        copy(hid_s.at[o], hid_s.at[o], send_h.at[0], recv_h.at[o], dp, z).wait_recv()
+    weights[5].wait()
+
+    @pl.loop(0, width // tw)
+    def _(i):
+        cols = pl.ds(pl.multiple_of(i * tw, tw), tw)
+        part = jnp.dot(
+            hid_s[...].reshape(ndp * 2 * cap, hs), sd[:, cols], preferred_element_type=jnp.float32
+        )
+        down_s[:, :, :, cols] = part.astype(jnp.bfloat16).reshape(ndp, 2, cap, tw)
+
+    for i, o in enumerate(others):
+        send(None, lambda i=i, o=o: copy(
+            down_s.at[o], gotd_s.at[dp], send_d.at[i], recv_d.at[dp], o, z))
+    gotd_s[dp] = down_s[dp]
+    for o in others:
+        copy(gotd_s.at[o], gotd_s.at[o], send_d.at[0], recv_d.at[o], dp, z).wait_recv()
+    copy(pair_e, row_e, send_py, recv_py, dp, z).wait_recv()
+
+    def own_sum(t, e, cols):
+        shared = gotd_s[t, e, :, cols].astype(jnp.float32)
+        near = part_e[dp, t, :, cols].astype(jnp.float32) + core_e[y, t, :, cols].astype(jnp.float32)
+        return shared + jnp.where(e == y, near, row_e[t, :, cols].astype(jnp.float32))
+
+    def combined(t, target, sources):
+        @pl.loop(0, per)
+        def _(i):
+            cols = pl.ds(pl.multiple_of(i * tw, tw), tw)
+            for e in range(2):
+                total = own_sum(t, e, cols)
+                for cond, ref in sources:
+                    total = total + jnp.where(cond, ref[t, e, :, cols].astype(jnp.float32), 0.0)
+                target[t, e, :, cols] = total.astype(jnp.bfloat16)
+
+    def arrive(ref, sems, t, cond):
+        @pl.when(cond)
+        def _():
+            copy(ref.at[t], ref.at[t], send_tr.at[t], sems.at[t], dp, z).wait_recv()
+
+        @pl.when(jnp.logical_not(cond))
+        def _():
+            ref[t] = jnp.zeros(ref.shape[1:], ref.dtype)
+
+    true = z >= 0
+    for i in range(nt - 1):
+        t = nt - 1 - i
+
+        @pl.when(t > z)
+        def _():
+            arrive(left, recv_tl, t, z > 0)
+            combined(t, passed, ((true, left),))
+
+        send(t > z, lambda t=t: copy(
+            passed.at[t], left.at[t], send_tr.at[t], recv_tl.at[t], dp, z + 1))
+        u = i
+
+        @pl.when(u < z)
+        def _():
+            arrive(right, recv_tr, u, z < nt - 1)
+            combined(u, passed, ((true, right),))
+
+        send(u < z, lambda u=u: copy(
+            passed.at[u], right.at[u], send_tl.at[u], recv_tr.at[u], dp, z - 1))
+    arrive(left, recv_tl, z, z > 0)
+    arrive(right, recv_tr, z, z < nt - 1)
+    combined(z, passed, ((true, left), (true, right)))
+
+    @pl.loop(0, per)
+    def _(i):
+        cols = pl.ds(pl.multiple_of(i * tw, tw), tw)
+        slots = passed[z, :, :, cols].reshape(2 * cap, tw)
+        out[:, cols] = jnp.dot(unpick[...], slots, preferred_element_type=jnp.float32).astype(
+            jnp.bfloat16
+        )
+
+    for cond, make in sending:
+        if cond is None:
+            make().wait_send()
+        else:
+            pl.when(cond)(lambda make=make: make().wait_send())
+
+
+def fused(tokens, router, eg, eu, ed, sg, su, sd, ids, slots):
+    ndp, nt = lax.axis_size("dp"), lax.axis_size("tensor")
+    tok_rows, width = tokens.shape
+    cap = min(2 * tok_rows // 2, tok_rows // 2)
+    spot = ids * cap + slots
+    pick = (jnp.arange(2 * cap, dtype=jnp.int32)[:, None] == spot[None, :]).astype(jnp.bfloat16)
+    unpick = (spot[:, None] == jnp.arange(2 * cap, dtype=jnp.int32)[None, :]).astype(jnp.bfloat16)
+    bf, f32 = jnp.bfloat16, jnp.float32
+    rows, hid, hs, depth = ndp * cap, eg.shape[1], sg.shape[1], eg.shape[0]
+    v = pltpu.VMEM
+    dma = pltpu.SemaphoreType.DMA
+    scratch = [v(w.shape, bf) for w in (eg, eu, ed, sg, su, sd)] + [
+        v((2, cap, width), bf),
+        v((nt, ndp, cap, width), bf),
+        v((ndp, cap, width), bf),
+        v((rows, router.shape[1]), f32),
+        v((rows, hid), f32),
+        v((rows, hid), f32),
+        v((rows, hid), bf),
+        v((ndp, nt, cap, width), bf),
+        v((2, nt, cap, width), bf),
+        v((nt, cap, width), bf),
+        v((nt, cap, width), bf),
+        v((ndp, 2, 2, cap, hs), bf),
+        v((ndp - 1, 2, 2, cap, hs), bf),
+        v((ndp, 2 * cap, hs), bf),
+        v((ndp, 2, cap, width), bf),
+        v((ndp, 2, cap, width), bf),
+        v((nt, 2, cap, width), bf),
+        v((nt, 2, cap, width), bf),
+        v((nt, 2, cap, width), bf),
+    ]
+    sems = [
+        dma((6,)), dma(()), dma(()), dma(()), dma((ndp,)), dma((ndp,)), dma((ndp,)),
+        dma((nt, 2)), dma((nt, 2)), dma((nt, 2)), dma((nt, 2)), dma((nt, 2)),
+        dma((2,)), dma((2,)), dma(()), dma(()), dma((ndp,)), dma((ndp,)), dma((ndp,)), dma((ndp,)),
+        dma((ndp,)), dma((ndp,)), dma((nt,)), dma((nt,)), dma((nt,)), dma((nt,)),
+    ]
+    in_vmem = pl.BlockSpec(memory_space=v)
+    in_hbm = pl.BlockSpec(memory_space=pl.ANY)
+    return pl.pallas_call(
+        functools.partial(layer_kernel, (ndp, nt, cap, width)),
+        out_shape=jax.ShapeDtypeStruct(tokens.shape, bf),
+        in_specs=[in_vmem] * 4 + [in_hbm] * 6,
+        out_specs=in_vmem,
+        scratch_shapes=scratch + sems,
+        compiler_params=pltpu.CompilerParams(
+            collective_id=0, has_side_effects=True, vmem_limit_bytes=VMEM_BYTES
+        ),
+    )(tokens, pick, unpick, router, eg, eu, ed, sg, su, sd)
+
+
+def fits(mesh):
+    return mesh.shape["dp"] == mesh.shape["tensor"] and mesh.shape["dp"] // 2 == 2
+
+
 def solution(mesh):
     in_specs = (
         P(("group", "dp"), "tensor"),
@@ -94,5 +487,5 @@
     )
     out_specs = P(("group", "dp"), "tensor")
     return jax.shard_map(
-        on_device, mesh=mesh, in_specs=in_specs, out_specs=out_specs, check_vma=False
-    )
+        fused if fits(mesh) else on_device, mesh=mesh, in_specs=in_specs, out_specs=out_specs, check_vma=False
+    )

time: 434 us -> 147 us (0.34)
  waiting for transfers between devices: 341 us -> 0 us
  Pallas kernels: 0 us -> 141 us
  matrix products: 34.2 us -> 0 us
  blocking collectives: 27.8 us -> 0 us
  between operations: 13.6 us -> 0.01 us
  local copies, waits for them, and re-layouts: 11.8 us -> 4.01 us
    all_gather x5 -> x0, waiting for transfers between devices: 279 us -> none  [the longest x1 71.6 us: on_device(): lax.all_gather(shared_down, 'dp', axis=1, tiled=True)]
    pallas_call x0 -> x1, Pallas kernels: none -> 141 us  [fused(): pl.pallas_call(functools.partial(layer_kernel, (ndp, nt, cap, width)), ou...]
    reduce_scatter x2 -> x0, waiting for transfers between devices: 59.6 us -> none  [the longest x1 42.4 us: on_device(): lax.psum_scatter(expert_terms.astype(jnp.bfloat16), 'tensor', scatter_dim...]
    dot_general x5 -> x0, matrix products: 34.2 us -> none  [the longest x1 11.2 us: on_device(): jnp.dot(shared_hidden, lax.all_gather(shared_down, 'dp', axis=1, tiled=Tr...]
    all_to_all x2 -> x0, blocking collectives: 27.8 us -> none  [the longest x1 14.1 us: on_device(): lax.all_to_all(lax.psum_scatter(expert_terms.astype(jnp.bfloat16), 'tenso...]
    scatter x1 -> x0, local copies, waits for them, and re-layouts: 9.83 us -> none  [on_device(): outgoing = jnp.zeros((experts, capacity, part_width), jnp.bfloat16).at[ex...]
  transfers between devices with their start and end apart: 7 -> 0, of which waited for: 7 -> 0; matrix products, arithmetic and copies ran while one was open for 8% -> 0% of each run, Pallas kernels for 0% -> 0%
where the time goes in v1:
time: 147 us
  Pallas kernels  141 us (96%)
  local copies, waits for them, and re-layouts  4.01 us (3%)
    pallas_call x1, Pallas kernels, fused(): pl.pallas_call(functools.partial(layer_kernel, (ndp, nt, cap, width)), ou...  141 us
    unnamed x2, local copies, waits for them, and re-layouts  4.01 us

profile of v1, /device:TPU:1, one launch (start us, length us, event | category | flops | bytes accessed | tf_op | source)
XLA Modules:
  0.0 146.8 jit_solution(13166407543683292783)
XLA Ops:
  0.0 0.7 multiply_add_fusion
  0.7 0.7 fusion.1
  1.4 2.3 %copy.11.router = bf16[5120,2]{1,0:T(8,128)(2,1)} copy(bf16[5120,2]{0,1:T(2,128)(2,1)} %param.11) | data formatting | bytes 40960 | tf_op args[1]
  3.7 141.4 %shard_map.100 = bf16[128,1280]{1,0:T(8,128)(2,1)} custom-call(bf16[128,1280]{1,0:T(8,128)(2,1)} %tok.1, bf16[128,128]{1,0:T(8,128)(2,1)} %get-tuple-element.6.pick, bf16[128,128]{1,0:T(8,128)(2,1)} %get-tuple-element.5.unpick, bf16[5120,2]{1,0:T(8,128)(2,1)} %copy.11.router, bf16[5120,512]{1,0:T(8,128)(2,1)} %eg_hbm.1, bf16[5120,512]{1,0:T(8,128)(2,1)} %eu_hbm.1, ...), custom_call_target="tpu_custom_call" | custom-call | tf_op jit(solution)/shard_map/pallas_call | solution.py:459
  145.1 1.7 %copy.13 = bf16[128,1280]{1,0:T(8,128)(2,1)} copy(bf16[128,1280]{1,0:T(8,128)(2,1)} %shard_map.100) | data formatting | bytes 655360

commit v2 on v1

--- a/solution.py
+++ b/solution.py
@@ -222,8 +222,9 @@
             copy(block, block, send_c.at[zs, j], recv_c.at[zs, j], mate, z).wait_recv()
         depth = pl.ds(pl.multiple_of(zs * width, width), width)
         x = table.at[zs]
-        logit[...] += jnp.dot(
-            x[...].reshape(rows, width), router[depth, :], preferred_element_type=jnp.float32
+        logit[...] += lax.dot_general(
+            x[...].reshape(rows, width), router[:, depth], (((1,), (1,)), ((), ())),
+            preferred_element_type=jnp.float32,
         )
 
         @pl.loop(0, acc_g.shape[1] // te)
@@ -279,11 +280,12 @@
                 part = jnp.dot(
                     src[...].reshape(rows, width), w[:, cols], preferred_element_type=jnp.float32
                 )
-                part_s[:, k, e, :, cols] = part.astype(jnp.bfloat16).reshape(ndp, cap, ts)
-
-    for i, o in enumerate(others):
-        send(None, lambda i=i, o=o: copy(
-            part_s.at[o], got_s.at[i], send_gs.at[i], recv_gs.at[i], o, z))
+                part_s[:, e, k, :, cols] = part.astype(jnp.bfloat16).reshape(ndp, cap, ts)
+
+    for e in range(2):
+        for i, o in enumerate(others):
+            send(None, lambda i=i, o=o, e=e: copy(
+                part_s.at[o, e], got_s.at[i, e], send_gs.at[i, e], recv_gs.at[i, e], o, z))
 
     lanes = lax.broadcasted_iota(jnp.int32, logit.shape, 1)
     gating = jax.nn.sigmoid(jnp.sum(jnp.where(lanes == y, logit[...], 0.0), axis=1, keepdims=True))
@@ -306,22 +308,21 @@
         send(None, lambda j=j: copy(
             part_e.at[2 * j + 1 - c], core_e.at[j], send_pc.at[j], recv_pc.at[j], mate, z))
 
-    for i in range(ndp - 1):
-        copy(part_s.at[0], got_s.at[i], send_gs.at[i], recv_gs.at[i], dp, z).wait_recv()
-
-    @pl.loop(0, hs // ts)
-    def _(i):
-        cols = pl.ds(pl.multiple_of(i * ts, ts), ts)
-        total = part_s[dp, :, :, :, cols].astype(jnp.float32)
-        for k in range(ndp - 1):
-            total = total + got_s[k, :, :, :, cols].astype(jnp.float32)
-        hid_s[dp, :, cols] = (jax.nn.silu(total[0]) * total[1]).astype(jnp.bfloat16).reshape(
-            2 * cap, ts
-        )
-
-    for i, o in enumerate(others):
-        send(None, lambda i=i, o=o: copy(
-            hid_s.at[dp], hid_s.at[dp], send_h.at[i], recv_h.at[dp], o, z))
+    for e in range(2):
+        for i in range(ndp - 1):
+            copy(part_s.at[0, e], got_s.at[i, e], send_gs.at[i, e], recv_gs.at[i, e], dp, z).wait_recv()
+
+        @pl.loop(0, hs // ts)
+        def _(i, e=e):
+            cols = pl.ds(pl.multiple_of(i * ts, ts), ts)
+            total = part_s[dp, e, :, :, cols].astype(jnp.float32)
+            for k in range(ndp - 1):
+                total = total + got_s[k, e, :, :, cols].astype(jnp.float32)
+            hid_s[e, dp, :, cols] = (jax.nn.silu(total[0]) * total[1]).astype(jnp.bfloat16)
+
+        for i, o in enumerate(others):
+            send(None, lambda i=i, o=o, e=e: copy(
+                hid_s.at[e, dp], hid_s.at[e, dp], send_h.at[i, e], recv_h.at[dp, e], o, z))
 
     for j in range(2):
         copy(part_e.at[0], core_e.at[j], send_pc.at[j], recv_pc.at[j], dp, z).wait_recv()
@@ -333,24 +334,23 @@
 
     send(None, lambda: copy(pair_e, row_e, send_py, recv_py, across, z))
 
-    for o in others:
-        copy(hid_s.at[o], hid_s.at[o], send_h.at[0], recv_h.at[o], dp, z).wait_recv()
     weights[5].wait()
-
-    @pl.loop(0, width // tw)
-    def _(i):
-        cols = pl.ds(pl.multiple_of(i * tw, tw), tw)
-        part = jnp.dot(
-            hid_s[...].reshape(ndp * 2 * cap, hs), sd[:, cols], preferred_element_type=jnp.float32
-        )
-        down_s[:, :, :, cols] = part.astype(jnp.bfloat16).reshape(ndp, 2, cap, tw)
-
-    for i, o in enumerate(others):
-        send(None, lambda i=i, o=o: copy(
-            down_s.at[o], gotd_s.at[dp], send_d.at[i], recv_d.at[dp], o, z))
-    gotd_s[dp] = down_s[dp]
-    for o in others:
-        copy(gotd_s.at[o], gotd_s.at[o], send_d.at[0], recv_d.at[o], dp, z).wait_recv()
+    for e in range(2):
+        for o in others:
+            copy(hid_s.at[e, o], hid_s.at[e, o], send_h.at[0, e], recv_h.at[o, e], dp, z).wait_recv()
+
+        @pl.loop(0, width // tw)
+        def _(i, e=e):
+            cols = pl.ds(pl.multiple_of(i * tw, tw), tw)
+            part = jnp.dot(
+                hid_s[e].reshape(rows, hs), sd[:, cols], preferred_element_type=jnp.float32
+            )
+            down_s[:, e, :, cols] = part.astype(jnp.bfloat16).reshape(ndp, cap, tw)
+
+        for i, o in enumerate(others):
+            send(None, lambda i=i, o=o, e=e: copy(
+                down_s.at[o, e], gotd_s.at[dp, e], send_d.at[i, e], recv_d.at[dp, e], o, z))
+        gotd_s[dp, e] = down_s[dp, e]
     copy(pair_e, row_e, send_py, recv_py, dp, z).wait_recv()
 
     def own_sum(t, e, cols):
@@ -358,48 +358,50 @@
         near = part_e[dp, t, :, cols].astype(jnp.float32) + core_e[y, t, :, cols].astype(jnp.float32)
         return shared + jnp.where(e == y, near, row_e[t, :, cols].astype(jnp.float32))
 
-    def combined(t, target, sources):
+    def combined(t, e, sources):
         @pl.loop(0, per)
         def _(i):
             cols = pl.ds(pl.multiple_of(i * tw, tw), tw)
-            for e in range(2):
-                total = own_sum(t, e, cols)
-                for cond, ref in sources:
-                    total = total + jnp.where(cond, ref[t, e, :, cols].astype(jnp.float32), 0.0)
-                target[t, e, :, cols] = total.astype(jnp.bfloat16)
-
-    def arrive(ref, sems, t, cond):
+            total = own_sum(t, e, cols)
+            for ref in sources:
+                total = total + ref[t, e, :, cols].astype(jnp.float32)
+            passed[t, e, :, cols] = total.astype(jnp.bfloat16)
+
+    def arrive(ref, sems, t, e, cond):
         @pl.when(cond)
         def _():
-            copy(ref.at[t], ref.at[t], send_tr.at[t], sems.at[t], dp, z).wait_recv()
+            copy(ref.at[t, e], ref.at[t, e], send_tr.at[t, e], sems.at[t, e], dp, z).wait_recv()
 
         @pl.when(jnp.logical_not(cond))
         def _():
-            ref[t] = jnp.zeros(ref.shape[1:], ref.dtype)
-
-    true = z >= 0
+            ref[t, e] = jnp.zeros(ref.shape[2:], ref.dtype)
+
     for i in range(nt - 1):
-        t = nt - 1 - i
-
-        @pl.when(t > z)
-        def _():
-            arrive(left, recv_tl, t, z > 0)
-            combined(t, passed, ((true, left),))
-
-        send(t > z, lambda t=t: copy(
-            passed.at[t], left.at[t], send_tr.at[t], recv_tl.at[t], dp, z + 1))
-        u = i
-
-        @pl.when(u < z)
-        def _():
-            arrive(right, recv_tr, u, z < nt - 1)
-            combined(u, passed, ((true, right),))
-
-        send(u < z, lambda u=u: copy(
-            passed.at[u], right.at[u], send_tl.at[u], recv_tr.at[u], dp, z - 1))
-    arrive(left, recv_tl, z, z > 0)
-    arrive(right, recv_tr, z, z < nt - 1)
-    combined(z, passed, ((true, left), (true, right)))
+        for e in range(2):
+            if i == 0:
+                for o in others:
+                    copy(gotd_s.at[o, e], gotd_s.at[o, e], send_d.at[0, e], recv_d.at[o, e], dp, z).wait_recv()
+            t, u = nt - 1 - i, i
+
+            @pl.when(t > z)
+            def _():
+                arrive(left, recv_tl, t, e, z > 0)
+                combined(t, e, (left,))
+
+            send(t > z, lambda t=t, e=e: copy(
+                passed.at[t, e], left.at[t, e], send_tr.at[t, e], recv_tl.at[t, e], dp, z + 1))
+
+            @pl.when(u < z)
+            def _():
+                arrive(right, recv_tr, u, e, z < nt - 1)
+                combined(u, e, (right,))
+
+            send(u < z, lambda u=u, e=e: copy(
+                passed.at[u, e], right.at[u, e], send_tl.at[u, e], recv_tr.at[u, e], dp, z - 1))
+    for e in range(2):
+        arrive(left, recv_tl, z, e, z > 0)
+        arrive(right, recv_tr, z, e, z < nt - 1)
+        combined(z, e, (left, right))
 
     @pl.loop(0, per)
     def _(i):
@@ -441,7 +443,7 @@
         v((nt, cap, width), bf),
         v((ndp, 2, 2, cap, hs), bf),
         v((ndp - 1, 2, 2, cap, hs), bf),
-        v((ndp, 2 * cap, hs), bf),
+        v((2, ndp, cap, hs), bf),
         v((ndp, 2, cap, width), bf),
         v((ndp, 2, cap, width), bf),
         v((nt, 2, cap, width), bf),
@@ -451,8 +453,8 @@
     sems = [
         dma((6,)), dma(()), dma(()), dma(()), dma((ndp,)), dma((ndp,)), dma((ndp,)),
         dma((nt, 2)), dma((nt, 2)), dma((nt, 2)), dma((nt, 2)), dma((nt, 2)),
-        dma((2,)), dma((2,)), dma(()), dma(()), dma((ndp,)), dma((ndp,)), dma((ndp,)), dma((ndp,)),
-        dma((ndp,)), dma((ndp,)), dma((nt,)), dma((nt,)), dma((nt,)), dma((nt,)),
+        dma((2,)), dma((2,)), dma(()), dma(()),
+        *[dma((ndp, 2))] * 6, *[dma((nt, 2))] * 4,
     ]
     in_vmem = pl.BlockSpec(memory_space=v)
     in_hbm = pl.BlockSpec(memory_space=pl.ANY)
@@ -465,7 +467,7 @@
         compiler_params=pltpu.CompilerParams(
             collective_id=0, has_side_effects=True, vmem_limit_bytes=VMEM_BYTES
         ),
-    )(tokens, pick, unpick, router, eg, eu, ed, sg, su, sd)
+    )(tokens, pick, unpick, router.T, eg, eu, ed, sg, su, sd)
 
 
 def fits(mesh):

time: 147 us -> 142 us (0.966); the launches traced: 147 us -> 140 us
  Pallas kernels: 141 us -> 137 us
  local copies, waits for them, and re-layouts: 4.01 us -> 1.72 us
    pallas_call x1, Pallas kernels: 141 us -> 137 us  [fused(): pl.pallas_call(functools.partial(layer_kernel, (ndp, nt, cap, width)), ou...]
    unnamed x2 -> x1, local copies, waits for them, and re-layouts: 4.01 us -> 1.72 us
where the time goes in v2:
time: 142 us; the launch traced here: 140 us
  Pallas kernels  137 us (96%)
  local copies, waits for them, and re-layouts  1.72 us (1%)
    pallas_call x1, Pallas kernels, fused(): pl.pallas_call(functools.partial(layer_kernel, (ndp, nt, cap, width)), ou...  137 us

profile of v2, /device:TPU:1, one launch (start us, length us, event | category | flops | bytes accessed | tf_op | source)
XLA Modules:
  0.0 140.1 jit_solution(6803128927478919728)
XLA Ops:
  0.0 0.7 multiply_add_fusion
  0.7 0.7 fusion.1
  1.4 137.0 %shard_map.100 = bf16[128,1280]{1,0:T(8,128)(2,1)} custom-call(bf16[128,1280]{1,0:T(8,128)(2,1)} %tok.1, bf16[128,128]{1,0:T(8,128)(2,1)} %get-tuple-element.6.pick, bf16[128,128]{1,0:T(8,128)(2,1)} %get-tuple-element.5.unpick, bf16[2,5120]{1,0:T(2,128)(2,1)} %bitcast.1, bf16[5120,512]{1,0:T(8,128)(2,1)} %eg_hbm.1, bf16[5120,512]{1,0:T(8,128)(2,1)} %eu_hbm.1, ...), custom_call_target="tpu_custom_call" | custom-call | tf_op jit(solution)/shard_map/pallas_call | solution.py:461
  138.4 1.7 %copy.12 = bf16[128,1280]{1,0:T(8,128)(2,1)} copy(bf16[128,1280]{1,0:T(8,128)(2,1)} %shard_map.100) | data formatting | bytes 655360
